TPU v7x, 32 devices: a whole 2x2x4 slice. The times are simulated.
32 devices in a mesh: rows: 8 (over z, x), feat: 4 (over y, core).
Axes of the slice: x: 2, y: 2, z: 4, core: 2. Of those that a mesh axis runs over, the one named last changes fastest.
Arguments:
- tile_values: bfloat16 [2048, 256, 128], P('rows', 'feat'), may hold values from -6 to 6
- tile_blocks: int32 [2048, 256], P('rows', 'feat'), may hold values from 0 to 2047
- tile_counts: int32 [2048, 4], P('rows', 'feat'), may hold values from 1 to 64, as said below
- labels: int32 [2048], P('rows'), may hold values 0 or 1
- owner_rank: int32 [2048], P('rows'), may hold values from 0 to 7, as said below
- weights: float32 [8192, 128], P(('feat', 'rows')), may hold values from -0.09375 to 0.09375
Outputs:
- owned_margins: float32 [2048], P('rows')
- gradient: float32 [8192, 128], P(('feat', 'rows'))
- loss: float32 [], replicated
Inputs may be any that keep to these rules, and one draw needn't show every extreme that they name: `owner_rank`: within each aligned block of 256 examples, every owner is named by exactly 32 examples. `tile_counts`: in every aligned block of 256 examples, each shard's column holds at least one example with exactly 64 used slots.
All inputs are finite; a program needn't handle non-finite values. No bound on the sum of `labels` on one device may be relied on, other than what follows from the above.
Results may differ from a plain program's by a relative error of at most 0.003.
Values may be sent and summed in bfloat16 or wider, within the bound.
A program may use at most 64 MiB of HBM per device.

v0:
```python
import math
import jax
import jax.numpy as jnp
from jax import lax
from jax.sharding import PartitionSpec as P


def on_device(tile_values, tile_blocks, tile_counts, labels, owner_rank, weights):
    examples = tile_values.shape[0]
    slot_count = tile_values.shape[1]
    tile_width = tile_values.shape[2]
    peer_count = lax.axis_size("rows")
    per_owner = examples // peer_count
    w_half = weights.astype(jnp.bfloat16)
    weight_table = lax.all_gather(w_half, "rows", axis=0, tiled=True)
    owner_hits = (owner_rank[:, None] == jnp.arange(peer_count, dtype=jnp.int32)[None, :]).astype(
        jnp.int32
    )
    earlier = jnp.cumsum(owner_hits, axis=0) - owner_hits
    local_rank = jnp.sum(earlier * owner_hits, axis=1)
    position = owner_rank * per_owner + local_rank
    send_order = (
        jnp.zeros((examples,), jnp.int32).at[position].set(jnp.arange(examples, dtype=jnp.int32))
    )
    counts_here = tile_counts[:, 0]
    live_slot = jnp.arange(slot_count, dtype=jnp.int32)[None, :] < counts_here[:, None]
    picked = weight_table[tile_blocks]
    products = jnp.sum(tile_values.astype(jnp.float32) * picked.astype(jnp.float32), axis=2)
    partial_value = jnp.sum(jnp.where(live_slot, products, jnp.float32(0.0)), axis=1)
    margin = lax.psum(partial_value, "feat")
    label_float = labels.astype(jnp.float32)
    residual = jax.nn.sigmoid(margin) - label_float
    loss_terms = jnp.sum(jax.nn.softplus(margin) - label_float * margin)
    loss = lax.psum(loss_terms, "rows") / (examples * peer_count)
    resid_half = residual.astype(jnp.bfloat16)
    coefficient = jnp.where(live_slot, resid_half[:, None], jnp.zeros((), jnp.bfloat16))
    total_tiles = examples * slot_count
    block_rows = math.gcd(total_tiles, 1024)
    turn_count = total_tiles // block_rows
    flat_values = tile_values.reshape(turn_count, block_rows, tile_width)
    flat_blocks = tile_blocks.reshape(turn_count, block_rows)
    flat_coefficient = coefficient.reshape(turn_count, block_rows)
    row_count = weights.shape[0] * lax.axis_size("rows")
    candidates = jnp.arange(row_count, dtype=jnp.int32)

    def add_block(running, pieces):
        block_values, block_ids, block_coefficient = pieces
        matches = block_ids[:, None] == candidates[None, :]
        spread = jnp.where(matches, block_coefficient[:, None], jnp.zeros((), jnp.bfloat16))
        update = lax.dot_general(
            spread, block_values, (((0,), (0,)), ((), ())), preferred_element_type=jnp.float32
        )
        return (running + update, None)

    start_sum = jnp.zeros((row_count, tile_width), jnp.float32)
    summed, unused = lax.scan(add_block, start_sum, (flat_values, flat_blocks, flat_coefficient))
    gradient = lax.psum_scatter(summed, "rows", scatter_dimension=0, tiled=True)
    ordered = margin[send_order].reshape(peer_count, per_owner)
    owned_margins = lax.all_to_all(
        ordered, "rows", split_axis=0, concat_axis=0, tiled=True
    ).reshape(examples)
    return (owned_margins, gradient, loss)


def solution(mesh):
    in_specs = (
        P("rows", "feat", None),
        P("rows", "feat"),
        P("rows", "feat"),
        P("rows"),
        P("rows"),
        P(("feat", "rows"), None),
    )
    out_specs = (P("rows"), P(("feat", "rows"), None), P())
    return jax.shard_map(
        on_device, mesh=mesh, in_specs=in_specs, out_specs=out_specs, check_vma=False
    )
```

profile of v0, /device:TPU:0, one launch (start us, length us, event | category | flops | bytes accessed | tf_op | source)
XLA Modules:
  0.0 238.3 jit_solution(4810306240248693229)
XLA Ops:
  7.2 0.0 reduce-scatter.2.cloned.1.call-start
  7.2 0.9 compare_select_fusion
  8.1 0.9 copy.16
  9.0 0.9 convert_element_type.23
  9.9 33.0 %all_gather.3 = bf16[2048,128]{1,0:T(8,128)(2,1)S(1)} all-gather(bf16[256,128]{1,0:T(8,128)(2,1)S(1)} %convert_element_type.23), channel_id=1, replica_groups=mesh['rows'=8,'feat'=4] {'rows'}, dimensions={0}, use_global_device_ids=true | all-gather | bytes 589824 | tf_op jit(solution)/shard_map/all_gather | solution.py:15
  43.0 0.1 copy.14
  43.0 0.1 reshape.56
  43.2 57.4 %gather_fusion = bf16[16384,128]{1,0:T(8,128)(2,1)} fusion(bf16[2048,128]{1,0:T(8,128)(2,1)S(1)} %all_gather.3, s32[16384]{0:T(1024)S(1)} %broadcast_clamp_fusion), kind=kCustom, calls=%fused_computation | custom fusion | bytes 8454144 | tf_op jit(solution)/shard_map/gather | solution.py:27
  100.6 0.0 copy-start.2
  100.6 0.0 copy-start.3
  100.6 5.7 %fusion.15 = f32[256,64]{1,0:T(8,128)S(1)} fusion(bf16[256,64,128]{2,1,0:T(8,128)(2,1)} %bitcast.22, bf16[256,64,128]{2,1,0:T(8,128)(2,1)} %param.8), kind=kLoop, calls=%fused_computation.18 | loop fusion | flops 8372224 | bytes 8454144 | tf_op jit(solution)/shard_map/reduce_sum | solution.py:28
  106.3 0.0 copy-done.2
  106.3 0.2 select_reduce_fusion
  106.5 5.7 %psum.14 = f32[256]{0:T(256)S(1)} all-reduce(f32[256]{0:T(256)S(1)} %select_reduce_fusion), channel_id=1, replica_groups=mesh['rows'=8,'feat'=4] {'feat'}, use_global_device_ids=true, to_apply=%region_2.3 | all-reduce | flops 256 | bytes 2048 | tf_op jit(solution)/shard_map/psum | solution.py:30
  112.2 0.1 reshape.52
  112.3 0.0 copy-done.3
  112.3 0.6 fusion.20
  112.9 0.1 broadcast_in_dim.58
  113.0 0.1 broadcast_in_dim.59
  113.1 0.1 broadcast_in_dim.60
  113.2 0.5 broadcast.67
  113.7 0.7 reduce.11
  114.4 0.1 lt.56
  114.5 0.1 lt.57
  114.6 0.1 lt.58
  114.7 0.1 lt.54
  114.8 0.0 copy-start.1
  114.8 48.5 %while.11 = (s32[]{:T(128)}, f32[2048,128]{1,0:T(8,128)S(1)}, s32[16,1024]{1,0:T(8,128)S(1)}, bf16[16,1024]{1,0:T(8,128)(2,1)S(1)}, bf16[16,1024,128]{2,1,0:T(8,128)(2,1)}, /*index=5*/s32[]{:T(128)}, s32[]{:T(128)}) while((s32[]{:T(128)}, f32[2048,128]{1,0:T(8,128)S(1)}, s32[16,1024]{1,0:T(8,128)S(1)}, ...), condition=%wide.region_8.9_spmd.clone, body=%wide.region_7.8_spmd.clone.sunk | while | flops 541589504 | bytes 2377835 | solution.py:56
  114.9 3.0 %fusion.29 = f32[2048,128]{1,0:T(8,128)S(1)} fusion(s32[1024]{0:T(1024)S(1)} %bitcast.24, bf16[1024]{0:T(1024)(128)(2,1)S(1)} %dynamic-slice_reduce_fusion.2, f32[2048,128]{1,0:T(8,128)S(1)} %get-tuple-element.107, pred[]{:T(512)S(6)} %compare.3, bf16[16,1024,128]{2,1,0:T(8,128)(2,1)} %get-tuple-element.117, s32[]{:T(128)S(6)} %copy.20), kind=kOutput, calls=%fused_computation.8.clone.1 | convolution fusion | flops 541589504 | bytes 2365445 | tf_op jit(solution)/shard_map/while/body/eval_jaxpr/dot_general | solution.py:50
  117.9 3.0 %fusion.29 = f32[2048,128]{1,0:T(8,128)S(1)} fusion(s32[1024]{0:T(1024)S(1)} %bitcast.24, bf16[1024]{0:T(1024)(128)(2,1)S(1)} %dynamic-slice_reduce_fusion.2, f32[2048,128]{1,0:T(8,128)S(1)} %get-tuple-element.107, pred[]{:T(512)S(6)} %compare.3, bf16[16,1024,128]{2,1,0:T(8,128)(2,1)} %get-tuple-element.117, s32[]{:T(128)S(6)} %copy.20), kind=kOutput, calls=%fused_computation.8.clone.1 | convolution fusion | flops 541589504 | bytes 2365445 | tf_op jit(solution)/shard_map/while/body/eval_jaxpr/dot_general | solution.py:50
  120.9 3.0 %fusion.29 = f32[2048,128]{1,0:T(8,128)S(1)} fusion(s32[1024]{0:T(1024)S(1)} %bitcast.24, bf16[1024]{0:T(1024)(128)(2,1)S(1)} %dynamic-slice_reduce_fusion.2, f32[2048,128]{1,0:T(8,128)S(1)} %get-tuple-element.107, pred[]{:T(512)S(6)} %compare.3, bf16[16,1024,128]{2,1,0:T(8,128)(2,1)} %get-tuple-element.117, s32[]{:T(128)S(6)} %copy.20), kind=kOutput, calls=%fused_computation.8.clone.1 | convolution fusion | flops 541589504 | bytes 2365445 | tf_op jit(solution)/shard_map/while/body/eval_jaxpr/dot_general | solution.py:50
  123.9 3.0 %fusion.29 = f32[2048,128]{1,0:T(8,128)S(1)} fusion(s32[1024]{0:T(1024)S(1)} %bitcast.24, bf16[1024]{0:T(1024)(128)(2,1)S(1)} %dynamic-slice_reduce_fusion.2, f32[2048,128]{1,0:T(8,128)S(1)} %get-tuple-element.107, pred[]{:T(512)S(6)} %compare.3, bf16[16,1024,128]{2,1,0:T(8,128)(2,1)} %get-tuple-element.117, s32[]{:T(128)S(6)} %copy.20), kind=kOutput, calls=%fused_computation.8.clone.1 | convolution fusion | flops 541589504 | bytes 2365445 | tf_op jit(solution)/shard_map/while/body/eval_jaxpr/dot_general | solution.py:50
  127.0 3.0 %fusion.29 = f32[2048,128]{1,0:T(8,128)S(1)} fusion(s32[1024]{0:T(1024)S(1)} %bitcast.24, bf16[1024]{0:T(1024)(128)(2,1)S(1)} %dynamic-slice_reduce_fusion.2, f32[2048,128]{1,0:T(8,128)S(1)} %get-tuple-element.107, pred[]{:T(512)S(6)} %compare.3, bf16[16,1024,128]{2,1,0:T(8,128)(2,1)} %get-tuple-element.117, s32[]{:T(128)S(6)} %copy.20), kind=kOutput, calls=%fused_computation.8.clone.1 | convolution fusion | flops 541589504 | bytes 2365445 | tf_op jit(solution)/shard_map/while/body/eval_jaxpr/dot_general | solution.py:50
  130.0 3.0 %fusion.29 = f32[2048,128]{1,0:T(8,128)S(1)} fusion(s32[1024]{0:T(1024)S(1)} %bitcast.24, bf16[1024]{0:T(1024)(128)(2,1)S(1)} %dynamic-slice_reduce_fusion.2, f32[2048,128]{1,0:T(8,128)S(1)} %get-tuple-element.107, pred[]{:T(512)S(6)} %compare.3, bf16[16,1024,128]{2,1,0:T(8,128)(2,1)} %get-tuple-element.117, s32[]{:T(128)S(6)} %copy.20), kind=kOutput, calls=%fused_computation.8.clone.1 | convolution fusion | flops 541589504 | bytes 2365445 | tf_op jit(solution)/shard_map/while/body/eval_jaxpr/dot_general | solution.py:50
  133.0 3.0 %fusion.29 = f32[2048,128]{1,0:T(8,128)S(1)} fusion(s32[1024]{0:T(1024)S(1)} %bitcast.24, bf16[1024]{0:T(1024)(128)(2,1)S(1)} %dynamic-slice_reduce_fusion.2, f32[2048,128]{1,0:T(8,128)S(1)} %get-tuple-element.107, pred[]{:T(512)S(6)} %compare.3, bf16[16,1024,128]{2,1,0:T(8,128)(2,1)} %get-tuple-element.117, s32[]{:T(128)S(6)} %copy.20), kind=kOutput, calls=%fused_computation.8.clone.1 | convolution fusion | flops 541589504 | bytes 2365445 | tf_op jit(solution)/shard_map/while/body/eval_jaxpr/dot_general | solution.py:50
  136.1 3.0 %fusion.29 = f32[2048,128]{1,0:T(8,128)S(1)} fusion(s32[1024]{0:T(1024)S(1)} %bitcast.24, bf16[1024]{0:T(1024)(128)(2,1)S(1)} %dynamic-slice_reduce_fusion.2, f32[2048,128]{1,0:T(8,128)S(1)} %get-tuple-element.107, pred[]{:T(512)S(6)} %compare.3, bf16[16,1024,128]{2,1,0:T(8,128)(2,1)} %get-tuple-element.117, s32[]{:T(128)S(6)} %copy.20), kind=kOutput, calls=%fused_computation.8.clone.1 | convolution fusion | flops 541589504 | bytes 2365445 | tf_op jit(solution)/shard_map/while/body/eval_jaxpr/dot_general | solution.py:50
  139.1 3.0 %fusion.29 = f32[2048,128]{1,0:T(8,128)S(1)} fusion(s32[1024]{0:T(1024)S(1)} %bitcast.24, bf16[1024]{0:T(1024)(128)(2,1)S(1)} %dynamic-slice_reduce_fusion.2, f32[2048,128]{1,0:T(8,128)S(1)} %get-tuple-element.107, pred[]{:T(512)S(6)} %compare.3, bf16[16,1024,128]{2,1,0:T(8,128)(2,1)} %get-tuple-element.117, s32[]{:T(128)S(6)} %copy.20), kind=kOutput, calls=%fused_computation.8.clone.1 | convolution fusion | flops 541589504 | bytes 2365445 | tf_op jit(solution)/shard_map/while/body/eval_jaxpr/dot_general | solution.py:50
  142.1 3.0 %fusion.29 = f32[2048,128]{1,0:T(8,128)S(1)} fusion(s32[1024]{0:T(1024)S(1)} %bitcast.24, bf16[1024]{0:T(1024)(128)(2,1)S(1)} %dynamic-slice_reduce_fusion.2, f32[2048,128]{1,0:T(8,128)S(1)} %get-tuple-element.107, pred[]{:T(512)S(6)} %compare.3, bf16[16,1024,128]{2,1,0:T(8,128)(2,1)} %get-tuple-element.117, s32[]{:T(128)S(6)} %copy.20), kind=kOutput, calls=%fused_computation.8.clone.1 | convolution fusion | flops 541589504 | bytes 2365445 | tf_op jit(solution)/shard_map/while/body/eval_jaxpr/dot_general | solution.py:50
  145.2 3.0 %fusion.29 = f32[2048,128]{1,0:T(8,128)S(1)} fusion(s32[1024]{0:T(1024)S(1)} %bitcast.24, bf16[1024]{0:T(1024)(128)(2,1)S(1)} %dynamic-slice_reduce_fusion.2, f32[2048,128]{1,0:T(8,128)S(1)} %get-tuple-element.107, pred[]{:T(512)S(6)} %compare.3, bf16[16,1024,128]{2,1,0:T(8,128)(2,1)} %get-tuple-element.117, s32[]{:T(128)S(6)} %copy.20), kind=kOutput, calls=%fused_computation.8.clone.1 | convolution fusion | flops 541589504 | bytes 2365445 | tf_op jit(solution)/shard_map/while/body/eval_jaxpr/dot_general | solution.py:50
  148.2 3.0 %fusion.29 = f32[2048,128]{1,0:T(8,128)S(1)} fusion(s32[1024]{0:T(1024)S(1)} %bitcast.24, bf16[1024]{0:T(1024)(128)(2,1)S(1)} %dynamic-slice_reduce_fusion.2, f32[2048,128]{1,0:T(8,128)S(1)} %get-tuple-element.107, pred[]{:T(512)S(6)} %compare.3, bf16[16,1024,128]{2,1,0:T(8,128)(2,1)} %get-tuple-element.117, s32[]{:T(128)S(6)} %copy.20), kind=kOutput, calls=%fused_computation.8.clone.1 | convolution fusion | flops 541589504 | bytes 2365445 | tf_op jit(solution)/shard_map/while/body/eval_jaxpr/dot_general | solution.py:50
  151.2 3.0 %fusion.29 = f32[2048,128]{1,0:T(8,128)S(1)} fusion(s32[1024]{0:T(1024)S(1)} %bitcast.24, bf16[1024]{0:T(1024)(128)(2,1)S(1)} %dynamic-slice_reduce_fusion.2, f32[2048,128]{1,0:T(8,128)S(1)} %get-tuple-element.107, pred[]{:T(512)S(6)} %compare.3, bf16[16,1024,128]{2,1,0:T(8,128)(2,1)} %get-tuple-element.117, s32[]{:T(128)S(6)} %copy.20), kind=kOutput, calls=%fused_computation.8.clone.1 | convolution fusion | flops 541589504 | bytes 2365445 | tf_op jit(solution)/shard_map/while/body/eval_jaxpr/dot_general | solution.py:50
  154.3 3.0 %fusion.29 = f32[2048,128]{1,0:T(8,128)S(1)} fusion(s32[1024]{0:T(1024)S(1)} %bitcast.24, bf16[1024]{0:T(1024)(128)(2,1)S(1)} %dynamic-slice_reduce_fusion.2, f32[2048,128]{1,0:T(8,128)S(1)} %get-tuple-element.107, pred[]{:T(512)S(6)} %compare.3, bf16[16,1024,128]{2,1,0:T(8,128)(2,1)} %get-tuple-element.117, s32[]{:T(128)S(6)} %copy.20), kind=kOutput, calls=%fused_computation.8.clone.1 | convolution fusion | flops 541589504 | bytes 2365445 | tf_op jit(solution)/shard_map/while/body/eval_jaxpr/dot_general | solution.py:50
  157.3 3.0 %fusion.29 = f32[2048,128]{1,0:T(8,128)S(1)} fusion(s32[1024]{0:T(1024)S(1)} %bitcast.24, bf16[1024]{0:T(1024)(128)(2,1)S(1)} %dynamic-slice_reduce_fusion.2, f32[2048,128]{1,0:T(8,128)S(1)} %get-tuple-element.107, pred[]{:T(512)S(6)} %compare.3, bf16[16,1024,128]{2,1,0:T(8,128)(2,1)} %get-tuple-element.117, s32[]{:T(128)S(6)} %copy.20), kind=kOutput, calls=%fused_computation.8.clone.1 | convolution fusion | flops 541589504 | bytes 2365445 | tf_op jit(solution)/shard_map/while/body/eval_jaxpr/dot_general | solution.py:50
  160.3 3.0 %fusion.29 = f32[2048,128]{1,0:T(8,128)S(1)} fusion(s32[1024]{0:T(1024)S(1)} %bitcast.24, bf16[1024]{0:T(1024)(128)(2,1)S(1)} %dynamic-slice_reduce_fusion.2, f32[2048,128]{1,0:T(8,128)S(1)} %get-tuple-element.107, pred[]{:T(512)S(6)} %compare.3, bf16[16,1024,128]{2,1,0:T(8,128)(2,1)} %get-tuple-element.117, s32[]{:T(128)S(6)} %copy.20), kind=kOutput, calls=%fused_computation.8.clone.1 | convolution fusion | flops 541589504 | bytes 2365445 | tf_op jit(solution)/shard_map/while/body/eval_jaxpr/dot_general | solution.py:50
  163.3 0.0 copy-start
  163.3 1.0 copy-done
  164.3 0.0 reduce-scatter.2.cloned.1.call-update
  164.3 0.0 copy-done.1
  164.3 0.6 reduce-window.6
  164.9 0.2 slice_reduce_fusion
  165.2 0.1 fusion.17
  165.3 1.4 scatter_custom_fusion
  166.7 1.9 gather_fusion.1
  168.7 0.7 all_to_all.6
  169.4 5.6 %all-to-all-start = ((f32[8,1,32]{2,1,0:T(1,128)}), f32[8,1,32]{2,1,0:T(1,128)S(1)}, u32[]{:S(2)}, u32[]{:S(2)}) async-start(f32[8,1,32]{2,1,0:T(1,128)} %all_to_all.6), calls=%async_computation | async-start | bytes 8192 | tf_op jit(solution)/shard_map/all_to_all | solution.py:59
  175.0 22.5 %psum.15 = f32[]{:T(128)} all-reduce(f32[]{:T(128)} %get-tuple-element.66), channel_id=1, replica_groups=mesh['rows'=8,'feat'=4] {'rows'}, use_global_device_ids=true, to_apply=%region_11.12 | all-reduce | flops 1 | bytes 8 | tf_op jit(solution)/shard_map/psum | solution.py:34
  198.1 0.0 all-to-all-done
  198.1 0.5 broadcast.66
  198.6 0.7 reduce.10
  199.3 0.6 reshape.51
  199.9 30.4 %reduce-scatter.2.cloned.1.call-done = f32[256,128]{1,0:T(8,128)} async-done(((f32[2048,128]{1,0:T(8,128)}), f32[256,128]{1,0:T(8,128)}) %reduce-scatter.2.cloned.1.call-update) | async-done | bytes 131088 | tf_op jit(solution)/shard_map/reduce_scatter | solution.py:57
  (43 shorter events, 0.8 us)
Async XLA Ops:
  7.2 223.2 %reduce-scatter.2.cloned.1.call-start = ((), (), s32[]{:S(2)}) async-start(), calls=%async_computation.2 | async-start | bytes 1179648 | tf_op jit(solution)/shard_map/reduce_scatter | solution.py:57
  100.6 5.7 %copy-start.2 = (s32[256,1]{0,1:T(1,128)S(1)}, s32[256,1]{0,1:T(1,128)}, u32[]{:S(2)}) copy-start(s32[256,1]{0,1:T(1,128)} %param.10) | copy-start | bytes 3076
  100.6 11.7 %copy-start.3 = (s32[256]{0:T(256)S(1)}, s32[256]{0:T(256)}, u32[]{:S(2)}) copy-start(s32[256]{0:T(256)} %param.11) | copy-start | bytes 3076
  114.8 49.5 %copy-start.1 = (s32[256]{0:T(256)S(1)}, s32[256]{0:T(256)}, u32[]{:S(2)}) copy-start(s32[256]{0:T(256)} %param.12) | copy-start | bytes 3076
  163.3 1.0 copy-start
  169.4 28.7 %all-to-all-start = ((f32[8,1,32]{2,1,0:T(1,128)}), f32[8,1,32]{2,1,0:T(1,128)S(1)}, u32[]{:S(2)}, u32[]{:S(2)}) async-start(f32[8,1,32]{2,1,0:T(1,128)} %all_to_all.6), calls=%async_computation | async-start | bytes 8192 | tf_op jit(solution)/shard_map/all_to_all | solution.py:59
Sparse Core Ops, SparseCore 0:
  164.4 65.8 reduce-scatter.1
where the time goes:
time: 239 us; the launch traced here: 238 us
  local copies, waits for them, and re-layouts  66.9 us (28%)
  blocking collectives  61.2 us (26%)
  matrix products  47.2 us (20%)
  waiting for transfers between devices  30.4 us (13%)
  between operations  16 us (7%)
  other arithmetic  10.4 us (4%)
  starting transfers between devices  5.66 us (2%)
    gather x1, local copies, waits for them, and re-layouts, on_device(): picked = weight_table[tile_blocks]  57.4 us
    dot_general x16, matrix products, add_block(): lax.dot_general(spread, block_values, (((0,), (0,)), ((), ())), preferred...  47.2 us
    all_gather x1, blocking collectives, on_device(): weight_table = lax.all_gather(w_half, 'rows', axis=0, tiled=True)  33 us
    reduce_scatter x1, waiting for transfers between devices, on_device(): gradient = lax.psum_scatter(summed, 'rows', scatter_dimension=0, tiled=True)  30.4 us
    psum x1, blocking collectives, on_device(): loss = lax.psum(loss_terms, 'rows') / (examples * peer_count)  22.5 us
    reduce_sum x1, other arithmetic, on_device(): jnp.sum(tile_values.astype(jnp.float32) * picked.astype(jnp.float32), axi...  5.72 us
    psum x1, blocking collectives, on_device(): margin = lax.psum(partial_value, 'feat')  5.66 us
    all_to_all x1, starting transfers between devices, on_device(): lax.all_to_all(ordered, 'rows', split_axis=0, concat_axis=0, tiled=True)  5.62 us
  transfers between devices with their start and end apart: 2, of which 1 were waited for; matrix products, arithmetic and copies ran while one was open for 3% of the time, Pallas kernels for 0%

commit v1 on v0

--- a/solution.py
+++ b/solution.py
@@ -12,7 +12,14 @@
     peer_count = lax.axis_size("rows")
     per_owner = examples // peer_count
     w_half = weights.astype(jnp.bfloat16)
-    weight_table = lax.all_gather(w_half, "rows", axis=0, tiled=True)
+    size = lax.axis_size("rows")
+    hops = [(i, (i + 1) % size) for i in range(size)]
+    parts = [w_half]
+    for far in range(1, size):
+        parts = [lax.ppermute(parts[0], "rows", hops), *parts]
+    whole = jnp.concatenate(parts, axis=0)
+    shift = (lax.axis_index("rows") + 1) * parts[-1].shape[0]
+    weight_table = jnp.roll(whole, shift, axis=0)
     owner_hits = (owner_rank[:, None] == jnp.arange(peer_count, dtype=jnp.int32)[None, :]).astype(
         jnp.int32
     )

time: 239 us -> 252 us (1.054)
  waiting for transfers between devices: 30.4 us -> 72.8 us
  blocking collectives: 61.2 us -> 28.1 us
    ppermute x0 -> x7, waiting for transfers between devices: none -> 43 us  [on_device(): parts = [lax.ppermute(parts[0], 'rows', hops), *parts]]
    all_gather x1 -> x0, blocking collectives: 33 us -> none  [on_device(): weight_table = lax.all_gather(w_half, 'rows', axis=0, tiled=True)]
    ppermute x0 -> x7, starting transfers between devices: none -> 2.98 us  [on_device(): parts = [lax.ppermute(parts[0], 'rows', hops), *parts]]
  transfers between devices with their start and end apart: 2 -> 9, of which waited for: 1 -> 8; matrix products, arithmetic and copies ran while one was open for 3% -> 4% of each run, Pallas kernels for 0% -> 0%
where the time goes in v1:
time: 252 us; the launch traced here: 251 us
  waiting for transfers between devices  72.8 us (29%)
  local copies, waits for them, and re-layouts  67 us (27%)
  matrix products  47 us (19%)
  blocking collectives  28.1 us (11%)
  between operations  16.1 us (6%)
  other arithmetic  12.9 us (5%)
  starting transfers between devices  6.35 us (3%)
    gather x1, local copies, waits for them, and re-layouts, on_device(): picked = weight_table[tile_blocks]  57.4 us
    dot_general x16, matrix products, add_block(): lax.dot_general(spread, block_values, (((0,), (0,)), ((), ())), preferred...  47 us
    ppermute x7, waiting for transfers between devices, on_device(): parts = [lax.ppermute(parts[0], 'rows', hops), *parts]  43 us
    reduce_scatter x1, waiting for transfers between devices, on_device(): gradient = lax.psum_scatter(summed, 'rows', scatter_dimension=0, tiled=True)  29.8 us
    psum x1, blocking collectives, on_device(): loss = lax.psum(loss_terms, 'rows') / (examples * peer_count)  22.4 us
    reduce_sum x1, other arithmetic, on_device(): jnp.sum(tile_values.astype(jnp.float32) * picked.astype(jnp.float32), axi...  5.72 us
    psum x1, blocking collectives, on_device(): margin = lax.psum(partial_value, 'feat')  5.66 us
  transfers between devices with their start and end apart: 9, of which 8 were waited for; matrix products, arithmetic and copies ran while one was open for 4% of the time, Pallas kernels for 0%

profile of v1, /device:TPU:0, one launch (start us, length us, event | category | flops | bytes accessed | tf_op | source)
XLA Modules:
  0.0 250.9 jit_solution(12156957905700008809)
XLA Ops:
  7.2 0.0 reduce-scatter.2.cloned.1.call-start
  7.2 0.9 convert_element_type.23
  8.1 3.0 %collective-permute-start = (bf16[256,128]{1,0:T(8,128)(2,1)S(1)}, bf16[256,128]{1,0:T(8,128)(2,1)S(1)}, u32[]{:S(2)}, u32[]{:S(2)}) collective-permute-start(bf16[256,128]{1,0:T(8,128)(2,1)S(1)} %convert_element_type.23), channel_id=1, source_target_pairs={{0,4},{4,8},{8,12},{12,16},{16,20},{20,24},{24,28},{28,0},{1,5},{5... | collective-permute-start | bytes 196616 | tf_op jit(solution)/shard_map/ppermute | solution.py:19
  11.1 5.3 %collective-permute-done = bf16[256,128]{1,0:T(8,128)(2,1)S(1)} collective-permute-done((bf16[256,128]{1,0:T(8,128)(2,1)S(1)}, bf16[256,128]{1,0:T(8,128)(2,1)S(1)}, u32[]{:S(2)}, u32[]{:S(2)}) %collective-permute-start) | collective-permute-done | bytes 65568 | tf_op jit(solution)/shard_map/ppermute | solution.py:19
  16.4 0.0 collective-permute-start.1
  16.4 7.0 %collective-permute-done.1 = bf16[256,128]{1,0:T(8,128)(2,1)S(1)} collective-permute-done((bf16[256,128]{1,0:T(8,128)(2,1)S(1)}, bf16[256,128]{1,0:T(8,128)(2,1)S(1)}, u32[]{:S(2)}, u32[]{:S(2)}) %collective-permute-start.1) | collective-permute-done | bytes 65568 | tf_op jit(solution)/shard_map/ppermute | solution.py:19
  23.3 7.0 %collective-permute-done.2 = bf16[256,128]{1,0:T(8,128)(2,1)S(1)} collective-permute-done((bf16[256,128]{1,0:T(8,128)(2,1)S(1)}, bf16[256,128]{1,0:T(8,128)(2,1)S(1)}, u32[]{:S(2)}, u32[]{:S(2)}) %collective-permute-start.2) | collective-permute-done | bytes 65568 | tf_op jit(solution)/shard_map/ppermute | solution.py:19
  30.3 7.0 %collective-permute-done.3 = bf16[256,128]{1,0:T(8,128)(2,1)S(1)} collective-permute-done((bf16[256,128]{1,0:T(8,128)(2,1)S(1)}, bf16[256,128]{1,0:T(8,128)(2,1)S(1)}, u32[]{:S(2)}, u32[]{:S(2)}) %collective-permute-start.3) | collective-permute-done | bytes 65568 | tf_op jit(solution)/shard_map/ppermute | solution.py:19
  37.3 7.3 %collective-permute-done.4 = bf16[256,128]{1,0:T(8,128)(2,1)S(1)} collective-permute-done((bf16[256,128]{1,0:T(8,128)(2,1)S(1)}, bf16[256,128]{1,0:T(8,128)(2,1)S(1)}, u32[]{:S(2)}, u32[]{:S(2)}) %collective-permute-start.4) | collective-permute-done | bytes 65568 | tf_op jit(solution)/shard_map/ppermute | solution.py:19
  44.6 0.8 compare_select_fusion
  45.4 0.1 copy.14
  45.5 0.1 reshape.56
  45.6 5.9 %collective-permute-done.5 = bf16[256,128]{1,0:T(8,128)(2,1)S(1)} collective-permute-done((bf16[256,128]{1,0:T(8,128)(2,1)S(1)}, bf16[256,128]{1,0:T(8,128)(2,1)S(1)}, u32[]{:S(2)}, u32[]{:S(2)}) %collective-permute-start.5) | collective-permute-done | bytes 65568 | tf_op jit(solution)/shard_map/ppermute | solution.py:19
  51.6 0.9 copy.16
  52.5 0.5 broadcast.68
  53.0 1.3 reduce.11
  54.4 0.1 lt.70
  54.5 0.1 lt.71
  54.6 0.1 lt.72
  54.7 0.1 lt.68
  54.7 0.1 reshape.52
  54.8 3.7 %collective-permute-done.6 = bf16[256,128]{1,0:T(8,128)(2,1)S(1)} collective-permute-done((bf16[256,128]{1,0:T(8,128)(2,1)S(1)}, bf16[256,128]{1,0:T(8,128)(2,1)S(1)}, u32[]{:S(2)}, u32[]{:S(2)}) %collective-permute-start.6) | collective-permute-done | bytes 65568 | tf_op jit(solution)/shard_map/ppermute | solution.py:19
  58.6 0.9 constant_dynamic-update-slice_fusion.8
  59.7 0.9 constant_dynamic-update-slice_fusion
  60.6 57.4 %gather_fusion = bf16[16384,128]{1,0:T(8,128)(2,1)} fusion(bf16[2048,128]{1,0:T(8,128)(2,1)S(1)} %constant_dynamic-slice_fusion.1, s32[16384]{0:T(1024)S(1)} %broadcast_clamp_fusion), kind=kCustom, calls=%fused_computation | custom fusion | bytes 8454144 | tf_op jit(solution)/shard_map/gather | solution.py:34
  118.0 5.7 %fusion.15 = f32[256,64]{1,0:T(8,128)S(1)} fusion(bf16[256,64,128]{2,1,0:T(8,128)(2,1)} %bitcast.22, bf16[256,64,128]{2,1,0:T(8,128)(2,1)} %param.8), kind=kLoop, calls=%fused_computation.18 | loop fusion | flops 8372224 | bytes 8454144 | tf_op jit(solution)/shard_map/reduce_sum | solution.py:35
  123.8 0.2 select_reduce_fusion
  123.9 5.7 %psum.14 = f32[256]{0:T(256)S(1)} all-reduce(f32[256]{0:T(256)S(1)} %select_reduce_fusion), channel_id=1, replica_groups=mesh['rows'=8,'feat'=4] {'feat'}, use_global_device_ids=true, to_apply=%region_2.3 | all-reduce | flops 256 | bytes 2048 | tf_op jit(solution)/shard_map/psum | solution.py:37
  129.6 0.6 fusion.20
  130.2 0.1 broadcast_in_dim.58
  130.3 0.1 broadcast_in_dim.59
  130.4 0.1 broadcast_in_dim.60
  130.6 0.0 copy-start.1
  130.6 48.3 %while.11 = (s32[]{:T(128)}, f32[2048,128]{1,0:T(8,128)S(1)}, s32[16,1024]{1,0:T(8,128)S(1)}, bf16[16,1024]{1,0:T(8,128)(2,1)S(1)}, bf16[16,1024,128]{2,1,0:T(8,128)(2,1)}, /*index=5*/s32[]{:T(128)}, s32[]{:T(128)}) while((s32[]{:T(128)}, f32[2048,128]{1,0:T(8,128)S(1)}, s32[16,1024]{1,0:T(8,128)S(1)}, ...), condition=%wide.region_8.9_spmd.clone, body=%wide.region_7.8_spmd.clone.sunk | while | flops 541589504 | bytes 2378335 | solution.py:63
  130.6 2.9 %fusion.29 = f32[2048,128]{1,0:T(8,128)S(1)} fusion(s32[1024]{0:T(1024)S(1)} %bitcast.24, bf16[1024]{0:T(1024)(128)(2,1)S(1)} %dynamic-slice_reduce_fusion.2, f32[2048,128]{1,0:T(8,128)S(1)} %get-tuple-element.107, pred[]{:T(512)S(6)} %compare.4, bf16[16,1024,128]{2,1,0:T(8,128)(2,1)} %get-tuple-element.117, s32[]{:T(128)} %get-tuple-element.106), kind=kOutput, calls=%fused_computation.8.clone.1 | convolution fusion | flops 541589504 | bytes 2365953 | tf_op jit(solution)/shard_map/while/body/eval_jaxpr/dot_general | solution.py:57
  133.7 2.9 %fusion.29 = f32[2048,128]{1,0:T(8,128)S(1)} fusion(s32[1024]{0:T(1024)S(1)} %bitcast.24, bf16[1024]{0:T(1024)(128)(2,1)S(1)} %dynamic-slice_reduce_fusion.2, f32[2048,128]{1,0:T(8,128)S(1)} %get-tuple-element.107, pred[]{:T(512)S(6)} %compare.4, bf16[16,1024,128]{2,1,0:T(8,128)(2,1)} %get-tuple-element.117, s32[]{:T(128)} %get-tuple-element.106), kind=kOutput, calls=%fused_computation.8.clone.1 | convolution fusion | flops 541589504 | bytes 2365953 | tf_op jit(solution)/shard_map/while/body/eval_jaxpr/dot_general | solution.py:57
  136.7 2.9 %fusion.29 = f32[2048,128]{1,0:T(8,128)S(1)} fusion(s32[1024]{0:T(1024)S(1)} %bitcast.24, bf16[1024]{0:T(1024)(128)(2,1)S(1)} %dynamic-slice_reduce_fusion.2, f32[2048,128]{1,0:T(8,128)S(1)} %get-tuple-element.107, pred[]{:T(512)S(6)} %compare.4, bf16[16,1024,128]{2,1,0:T(8,128)(2,1)} %get-tuple-element.117, s32[]{:T(128)} %get-tuple-element.106), kind=kOutput, calls=%fused_computation.8.clone.1 | convolution fusion | flops 541589504 | bytes 2365953 | tf_op jit(solution)/shard_map/while/body/eval_jaxpr/dot_general | solution.py:57
  139.7 2.9 %fusion.29 = f32[2048,128]{1,0:T(8,128)S(1)} fusion(s32[1024]{0:T(1024)S(1)} %bitcast.24, bf16[1024]{0:T(1024)(128)(2,1)S(1)} %dynamic-slice_reduce_fusion.2, f32[2048,128]{1,0:T(8,128)S(1)} %get-tuple-element.107, pred[]{:T(512)S(6)} %compare.4, bf16[16,1024,128]{2,1,0:T(8,128)(2,1)} %get-tuple-element.117, s32[]{:T(128)} %get-tuple-element.106), kind=kOutput, calls=%fused_computation.8.clone.1 | convolution fusion | flops 541589504 | bytes 2365953 | tf_op jit(solution)/shard_map/while/body/eval_jaxpr/dot_general | solution.py:57
  142.7 2.9 %fusion.29 = f32[2048,128]{1,0:T(8,128)S(1)} fusion(s32[1024]{0:T(1024)S(1)} %bitcast.24, bf16[1024]{0:T(1024)(128)(2,1)S(1)} %dynamic-slice_reduce_fusion.2, f32[2048,128]{1,0:T(8,128)S(1)} %get-tuple-element.107, pred[]{:T(512)S(6)} %compare.4, bf16[16,1024,128]{2,1,0:T(8,128)(2,1)} %get-tuple-element.117, s32[]{:T(128)} %get-tuple-element.106), kind=kOutput, calls=%fused_computation.8.clone.1 | convolution fusion | flops 541589504 | bytes 2365953 | tf_op jit(solution)/shard_map/while/body/eval_jaxpr/dot_general | solution.py:57
  145.7 2.9 %fusion.29 = f32[2048,128]{1,0:T(8,128)S(1)} fusion(s32[1024]{0:T(1024)S(1)} %bitcast.24, bf16[1024]{0:T(1024)(128)(2,1)S(1)} %dynamic-slice_reduce_fusion.2, f32[2048,128]{1,0:T(8,128)S(1)} %get-tuple-element.107, pred[]{:T(512)S(6)} %compare.4, bf16[16,1024,128]{2,1,0:T(8,128)(2,1)} %get-tuple-element.117, s32[]{:T(128)} %get-tuple-element.106), kind=kOutput, calls=%fused_computation.8.clone.1 | convolution fusion | flops 541589504 | bytes 2365953 | tf_op jit(solution)/shard_map/while/body/eval_jaxpr/dot_general | solution.py:57
  148.7 2.9 %fusion.29 = f32[2048,128]{1,0:T(8,128)S(1)} fusion(s32[1024]{0:T(1024)S(1)} %bitcast.24, bf16[1024]{0:T(1024)(128)(2,1)S(1)} %dynamic-slice_reduce_fusion.2, f32[2048,128]{1,0:T(8,128)S(1)} %get-tuple-element.107, pred[]{:T(512)S(6)} %compare.4, bf16[16,1024,128]{2,1,0:T(8,128)(2,1)} %get-tuple-element.117, s32[]{:T(128)} %get-tuple-element.106), kind=kOutput, calls=%fused_computation.8.clone.1 | convolution fusion | flops 541589504 | bytes 2365953 | tf_op jit(solution)/shard_map/while/body/eval_jaxpr/dot_general | solution.py:57
  151.8 2.9 %fusion.29 = f32[2048,128]{1,0:T(8,128)S(1)} fusion(s32[1024]{0:T(1024)S(1)} %bitcast.24, bf16[1024]{0:T(1024)(128)(2,1)S(1)} %dynamic-slice_reduce_fusion.2, f32[2048,128]{1,0:T(8,128)S(1)} %get-tuple-element.107, pred[]{:T(512)S(6)} %compare.4, bf16[16,1024,128]{2,1,0:T(8,128)(2,1)} %get-tuple-element.117, s32[]{:T(128)} %get-tuple-element.106), kind=kOutput, calls=%fused_computation.8.clone.1 | convolution fusion | flops 541589504 | bytes 2365953 | tf_op jit(solution)/shard_map/while/body/eval_jaxpr/dot_general | solution.py:57
  154.8 2.9 %fusion.29 = f32[2048,128]{1,0:T(8,128)S(1)} fusion(s32[1024]{0:T(1024)S(1)} %bitcast.24, bf16[1024]{0:T(1024)(128)(2,1)S(1)} %dynamic-slice_reduce_fusion.2, f32[2048,128]{1,0:T(8,128)S(1)} %get-tuple-element.107, pred[]{:T(512)S(6)} %compare.4, bf16[16,1024,128]{2,1,0:T(8,128)(2,1)} %get-tuple-element.117, s32[]{:T(128)} %get-tuple-element.106), kind=kOutput, calls=%fused_computation.8.clone.1 | convolution fusion | flops 541589504 | bytes 2365953 | tf_op jit(solution)/shard_map/while/body/eval_jaxpr/dot_general | solution.py:57
  157.8 2.9 %fusion.29 = f32[2048,128]{1,0:T(8,128)S(1)} fusion(s32[1024]{0:T(1024)S(1)} %bitcast.24, bf16[1024]{0:T(1024)(128)(2,1)S(1)} %dynamic-slice_reduce_fusion.2, f32[2048,128]{1,0:T(8,128)S(1)} %get-tuple-element.107, pred[]{:T(512)S(6)} %compare.4, bf16[16,1024,128]{2,1,0:T(8,128)(2,1)} %get-tuple-element.117, s32[]{:T(128)} %get-tuple-element.106), kind=kOutput, calls=%fused_computation.8.clone.1 | convolution fusion | flops 541589504 | bytes 2365953 | tf_op jit(solution)/shard_map/while/body/eval_jaxpr/dot_general | solution.py:57
  160.8 2.9 %fusion.29 = f32[2048,128]{1,0:T(8,128)S(1)} fusion(s32[1024]{0:T(1024)S(1)} %bitcast.24, bf16[1024]{0:T(1024)(128)(2,1)S(1)} %dynamic-slice_reduce_fusion.2, f32[2048,128]{1,0:T(8,128)S(1)} %get-tuple-element.107, pred[]{:T(512)S(6)} %compare.4, bf16[16,1024,128]{2,1,0:T(8,128)(2,1)} %get-tuple-element.117, s32[]{:T(128)} %get-tuple-element.106), kind=kOutput, calls=%fused_computation.8.clone.1 | convolution fusion | flops 541589504 | bytes 2365953 | tf_op jit(solution)/shard_map/while/body/eval_jaxpr/dot_general | solution.py:57
  163.8 2.9 %fusion.29 = f32[2048,128]{1,0:T(8,128)S(1)} fusion(s32[1024]{0:T(1024)S(1)} %bitcast.24, bf16[1024]{0:T(1024)(128)(2,1)S(1)} %dynamic-slice_reduce_fusion.2, f32[2048,128]{1,0:T(8,128)S(1)} %get-tuple-element.107, pred[]{:T(512)S(6)} %compare.4, bf16[16,1024,128]{2,1,0:T(8,128)(2,1)} %get-tuple-element.117, s32[]{:T(128)} %get-tuple-element.106), kind=kOutput, calls=%fused_computation.8.clone.1 | convolution fusion | flops 541589504 | bytes 2365953 | tf_op jit(solution)/shard_map/while/body/eval_jaxpr/dot_general | solution.py:57
  166.8 2.9 %fusion.29 = f32[2048,128]{1,0:T(8,128)S(1)} fusion(s32[1024]{0:T(1024)S(1)} %bitcast.24, bf16[1024]{0:T(1024)(128)(2,1)S(1)} %dynamic-slice_reduce_fusion.2, f32[2048,128]{1,0:T(8,128)S(1)} %get-tuple-element.107, pred[]{:T(512)S(6)} %compare.4, bf16[16,1024,128]{2,1,0:T(8,128)(2,1)} %get-tuple-element.117, s32[]{:T(128)} %get-tuple-element.106), kind=kOutput, calls=%fused_computation.8.clone.1 | convolution fusion | flops 541589504 | bytes 2365953 | tf_op jit(solution)/shard_map/while/body/eval_jaxpr/dot_general | solution.py:57
  169.9 2.9 %fusion.29 = f32[2048,128]{1,0:T(8,128)S(1)} fusion(s32[1024]{0:T(1024)S(1)} %bitcast.24, bf16[1024]{0:T(1024)(128)(2,1)S(1)} %dynamic-slice_reduce_fusion.2, f32[2048,128]{1,0:T(8,128)S(1)} %get-tuple-element.107, pred[]{:T(512)S(6)} %compare.4, bf16[16,1024,128]{2,1,0:T(8,128)(2,1)} %get-tuple-element.117, s32[]{:T(128)} %get-tuple-element.106), kind=kOutput, calls=%fused_computation.8.clone.1 | convolution fusion | flops 541589504 | bytes 2365953 | tf_op jit(solution)/shard_map/while/body/eval_jaxpr/dot_general | solution.py:57
  172.9 2.9 %fusion.29 = f32[2048,128]{1,0:T(8,128)S(1)} fusion(s32[1024]{0:T(1024)S(1)} %bitcast.24, bf16[1024]{0:T(1024)(128)(2,1)S(1)} %dynamic-slice_reduce_fusion.2, f32[2048,128]{1,0:T(8,128)S(1)} %get-tuple-element.107, pred[]{:T(512)S(6)} %compare.4, bf16[16,1024,128]{2,1,0:T(8,128)(2,1)} %get-tuple-element.117, s32[]{:T(128)} %get-tuple-element.106), kind=kOutput, calls=%fused_computation.8.clone.1 | convolution fusion | flops 541589504 | bytes 2365953 | tf_op jit(solution)/shard_map/while/body/eval_jaxpr/dot_general | solution.py:57
  175.9 2.9 %fusion.29 = f32[2048,128]{1,0:T(8,128)S(1)} fusion(s32[1024]{0:T(1024)S(1)} %bitcast.24, bf16[1024]{0:T(1024)(128)(2,1)S(1)} %dynamic-slice_reduce_fusion.2, f32[2048,128]{1,0:T(8,128)S(1)} %get-tuple-element.107, pred[]{:T(512)S(6)} %compare.4, bf16[16,1024,128]{2,1,0:T(8,128)(2,1)} %get-tuple-element.117, s32[]{:T(128)} %get-tuple-element.106), kind=kOutput, calls=%fused_computation.8.clone.1 | convolution fusion | flops 541589504 | bytes 2365953 | tf_op jit(solution)/shard_map/while/body/eval_jaxpr/dot_general | solution.py:57
  178.9 1.0 copy-done
  179.8 0.0 reduce-scatter.2.cloned.1.call-update
  179.9 0.6 reduce-window.6
  180.5 0.2 slice_reduce_fusion
  180.7 0.1 fusion.17
  180.8 1.4 scatter_custom_fusion
  182.3 1.9 gather_fusion.1
  184.2 0.7 all_to_all.6
  184.9 3.3 %all-to-all-start = ((f32[8,1,32]{2,1,0:T(1,128)}), f32[8,1,32]{2,1,0:T(1,128)S(1)}, u32[]{:S(2)}, u32[]{:S(2)}) async-start(f32[8,1,32]{2,1,0:T(1,128)} %all_to_all.6), calls=%async_computation | async-start | bytes 8192 | tf_op jit(solution)/shard_map/all_to_all | solution.py:66
  188.2 22.4 %psum.15 = f32[]{:T(128)} all-reduce(f32[]{:T(128)} %get-tuple-element.66), channel_id=1, replica_groups=mesh['rows'=8,'feat'=4] {'rows'}, use_global_device_ids=true, to_apply=%region_11.12 | all-reduce | flops 1 | bytes 8 | tf_op jit(solution)/shard_map/psum | solution.py:41
  211.3 0.5 broadcast.67
  211.8 0.7 reduce.10
  212.5 0.6 reshape.51
  213.1 29.8 %reduce-scatter.2.cloned.1.call-done = f32[256,128]{1,0:T(8,128)} async-done(((f32[2048,128]{1,0:T(8,128)}), f32[256,128]{1,0:T(8,128)}) %reduce-scatter.2.cloned.1.call-update) | async-done | bytes 131088 | tf_op jit(solution)/shard_map/reduce_scatter | solution.py:64
  (70 shorter events, 1.0 us)
Async XLA Ops:
  7.2 235.7 %reduce-scatter.2.cloned.1.call-start = ((), (), s32[]{:S(2)}) async-start(), calls=%async_computation.2 | async-start | bytes 1179648 | tf_op jit(solution)/shard_map/reduce_scatter | solution.py:64
  8.1 8.2 %collective-permute-start = (bf16[256,128]{1,0:T(8,128)(2,1)S(1)}, bf16[256,128]{1,0:T(8,128)(2,1)S(1)}, u32[]{:S(2)}, u32[]{:S(2)}) collective-permute-start(bf16[256,128]{1,0:T(8,128)(2,1)S(1)} %convert_element_type.23), channel_id=1, source_target_pairs={{0,4},{4,8},{8,12},{12,16},{16,20},{20,24},{24,28},{28,0},{1,5},{5... | collective-permute-start | bytes 196616 | tf_op jit(solution)/shard_map/ppermute | solution.py:19
  16.4 7.0 %collective-permute-start.1 = (bf16[256,128]{1,0:T(8,128)(2,1)S(1)}, bf16[256,128]{1,0:T(8,128)(2,1)S(1)}, u32[]{:S(2)}, u32[]{:S(2)}) collective-permute-start(bf16[256,128]{1,0:T(8,128)(2,1)S(1)} %collective-permute-done), channel_id=1, source_target_pairs={{0,4},{4,8},{8,12},{12,16},{16,20},{20,24},{24,28},{28,0},{1,5},{5... | collective-permute-start | bytes 196616 | tf_op jit(solution)/shard_map/ppermute | solution.py:19
  23.3 7.0 %collective-permute-start.2 = (bf16[256,128]{1,0:T(8,128)(2,1)S(1)}, bf16[256,128]{1,0:T(8,128)(2,1)S(1)}, u32[]{:S(2)}, u32[]{:S(2)}) collective-permute-start(bf16[256,128]{1,0:T(8,128)(2,1)S(1)} %collective-permute-done.1), channel_id=1, source_target_pairs={{0,4},{4,8},{8,12},{12,16},{16,20},{20,24},{24,28},{28,0},{1,5},{5... | collective-permute-start | bytes 196616 | tf_op jit(solution)/shard_map/ppermute | solution.py:19
  30.3 7.0 %collective-permute-start.3 = (bf16[256,128]{1,0:T(8,128)(2,1)S(1)}, bf16[256,128]{1,0:T(8,128)(2,1)S(1)}, u32[]{:S(2)}, u32[]{:S(2)}) collective-permute-start(bf16[256,128]{1,0:T(8,128)(2,1)S(1)} %collective-permute-done.2), channel_id=1, source_target_pairs={{0,4},{4,8},{8,12},{12,16},{16,20},{20,24},{24,28},{28,0},{1,5},{5... | collective-permute-start | bytes 196616 | tf_op jit(solution)/shard_map/ppermute | solution.py:19
  37.3 7.3 %collective-permute-start.4 = (bf16[256,128]{1,0:T(8,128)(2,1)S(1)}, bf16[256,128]{1,0:T(8,128)(2,1)S(1)}, u32[]{:S(2)}, u32[]{:S(2)}) collective-permute-start(bf16[256,128]{1,0:T(8,128)(2,1)S(1)} %collective-permute-done.3), channel_id=1, source_target_pairs={{0,4},{4,8},{8,12},{12,16},{16,20},{20,24},{24,28},{28,0},{1,5},{5... | collective-permute-start | bytes 196616 | tf_op jit(solution)/shard_map/ppermute | solution.py:19
  44.6 7.0 %collective-permute-start.5 = (bf16[256,128]{1,0:T(8,128)(2,1)S(1)}, bf16[256,128]{1,0:T(8,128)(2,1)S(1)}, u32[]{:S(2)}, u32[]{:S(2)}) collective-permute-start(bf16[256,128]{1,0:T(8,128)(2,1)S(1)} %collective-permute-done.4), channel_id=1, source_target_pairs={{0,4},{4,8},{8,12},{12,16},{16,20},{20,24},{24,28},{28,0},{1,5},{5... | collective-permute-start | bytes 196616 | tf_op jit(solution)/shard_map/ppermute | solution.py:19
  51.5 7.0 %collective-permute-start.6 = (bf16[256,128]{1,0:T(8,128)(2,1)S(1)}, bf16[256,128]{1,0:T(8,128)(2,1)S(1)}, u32[]{:S(2)}, u32[]{:S(2)}) collective-permute-start(bf16[256,128]{1,0:T(8,128)(2,1)S(1)} %collective-permute-done.5), channel_id=1, source_target_pairs={{0,4},{4,8},{8,12},{12,16},{16,20},{20,24},{24,28},{28,0},{1,5},{5... | collective-permute-start | bytes 196616 | tf_op jit(solution)/shard_map/ppermute | solution.py:19
  118.0 5.7 %copy-start.2 = (s32[256,1]{0,1:T(1,128)S(1)}, s32[256,1]{0,1:T(1,128)}, u32[]{:S(2)}) copy-start(s32[256,1]{0,1:T(1,128)} %param.10) | copy-start | bytes 3076
  118.0 11.6 %copy-start.3 = (s32[256]{0:T(256)S(1)}, s32[256]{0:T(256)}, u32[]{:S(2)}) copy-start(s32[256]{0:T(256)} %param.11) | copy-start | bytes 3076
  130.6 49.3 %copy-start.1 = (s32[256]{0:T(256)S(1)}, s32[256]{0:T(256)}, u32[]{:S(2)}) copy-start(s32[256]{0:T(256)} %param.12) | copy-start | bytes 3076
  178.8 1.0 copy-start
  184.9 26.4 %all-to-all-start = ((f32[8,1,32]{2,1,0:T(1,128)}), f32[8,1,32]{2,1,0:T(1,128)S(1)}, u32[]{:S(2)}, u32[]{:S(2)}) async-start(f32[8,1,32]{2,1,0:T(1,128)} %all_to_all.6), calls=%async_computation | async-start | bytes 8192 | tf_op jit(solution)/shard_map/all_to_all | solution.py:66
Sparse Core Ops, SparseCore 0:
  180.0 62.8 reduce-scatter.1
